TPU v7x, 32 devices: a whole 2x2x4 slice. The times are simulated.
32 devices in a mesh: frame: 16 (over z, y, x), row: 2 (over core).
Axes of the slice: x: 2, y: 2, z: 4, core: 2. Of those that a mesh axis runs over, the one named last changes fastest.
Arguments:
- footage: float32 [64, 1024, 1024], P('frame', 'row'), may hold values from -30 to 30
Outputs:
- coefficients: float32 [64, 1024, 1024], P('frame', 'row')
- energies: float32 [4, 10], replicated
All inputs are finite; a program needn't handle non-finite values.
Results may differ from a plain program's by a relative error of at most 0.00007.
Values sent between devices are 32-bit elements; how exact they have to be, the bound alone decides.
A program may use at most 128 MiB of HBM per device.

v0:
```python
import jax
import jax.numpy as jnp
import numpy as np
from jax import lax
from jax.sharding import PartitionSpec as P

SLEVELS = 3
TLEVELS = 3
LIFT_ALPHA = -1.586134342
LIFT_BETA = -0.05298011854
LIFT_GAMMA = 0.8829110762
LIFT_DELTA = 0.4435068522
LIFT_ZETA = 1.149604398


def shifted(block, axis, distance):
    devices = range(lax.axis_size(axis))
    route = [(i - distance, i) for i in devices if i - distance in devices]
    return lax.ppermute(block, axis, route)


def mirror_after(values, along):
    length = values.shape[along]
    return jnp.concatenate(
        [
            lax.slice_in_dim(values, 1, length, axis=along),
            lax.slice_in_dim(values, length - 1, length, axis=along),
        ],
        axis=along,
    )


def mirror_before(values, along):
    length = values.shape[along]
    return jnp.concatenate(
        [
            lax.slice_in_dim(values, 0, 1, axis=along),
            lax.slice_in_dim(values, 0, length - 1, axis=along),
        ],
        axis=along,
    )


def weave_axis(even_part, odd_part, along):
    stacked = jnp.stack([even_part, odd_part], axis=along + 1)
    new_shape = list(even_part.shape)
    new_shape[along] = new_shape[along] * 2
    return stacked.reshape(tuple(new_shape))


def lift_pair(even_part, odd_part, take_next, take_prev):
    odd_part = odd_part + LIFT_ALPHA * (even_part + take_next(even_part))
    even_part = even_part + LIFT_BETA * (take_prev(odd_part) + odd_part)
    odd_part = odd_part + LIFT_GAMMA * (even_part + take_next(even_part))
    even_part = even_part + LIFT_DELTA * (take_prev(odd_part) + odd_part)
    return (even_part * LIFT_ZETA, odd_part * (1.0 / LIFT_ZETA))


def table_next(values):
    return np.concatenate([values[:, 1:], values[:, -1:]], axis=1)


def table_prev(values):
    return np.concatenate([values[:, :1], values[:, :-1]], axis=1)


def column_matrix(width):
    identity = np.eye(width)
    even_part = identity[:, 0::2]
    odd_part = identity[:, 1::2]
    odd_part = odd_part + LIFT_ALPHA * (even_part + table_next(even_part))
    even_part = even_part + LIFT_BETA * (table_prev(odd_part) + odd_part)
    odd_part = odd_part + LIFT_GAMMA * (even_part + table_next(even_part))
    even_part = even_part + LIFT_DELTA * (table_prev(odd_part) + odd_part)
    lifted = np.concatenate([even_part * LIFT_ZETA, odd_part * (1.0 / LIFT_ZETA)], axis=1)
    return jnp.asarray(lifted.astype(np.float32))


def spatial_inplace(block, levels):
    frame_count, row_count, width = block.shape
    mixed = jnp.dot(block, column_matrix(width), precision=lax.Precision.HIGHEST)
    paired = mixed.reshape(frame_count, row_count // 2, 2, width)
    low_rows, high_rows = lift_pair(paired[:, :, 0, :], paired[:, :, 1, :], rows_next, rows_prev)
    half_width = width // 2
    coarse = low_rows[..., :half_width]
    if levels > 1:
        coarse = spatial_inplace(coarse, levels - 1)
    upper_rows = weave_axis(coarse, low_rows[..., half_width:], 2)
    bottom = weave_axis(high_rows[..., :half_width], high_rows[..., half_width:], 2)
    return jnp.stack([upper_rows, bottom], axis=2).reshape(frame_count, row_count, width)


def temporal(planes_in, levels):
    even_part = planes_in[0::2]
    odd_part = planes_in[1::2]
    odd_part = odd_part - 0.5 * (even_part + mirror_after(even_part, 0))
    even_part = even_part + 0.25 * (mirror_before(odd_part, 0) + odd_part)
    if levels > 1:
        even_part = temporal(even_part, levels - 1)
    return weave_axis(even_part, odd_part, 0)


def rows_next(values):
    arrived = shifted(values[:, :1], "row", -1)
    is_last = lax.axis_index("row") == lax.axis_size("row") - 1
    return jnp.concatenate([values[:, 1:], jnp.where(is_last, values[:, -1:], arrived)], axis=1)


def rows_prev(values):
    arrived = shifted(values[:, -1:], "row", 1)
    is_first = lax.axis_index("row") == 0
    return jnp.concatenate([jnp.where(is_first, values[:, :1], arrived), values[:, :-1]], axis=1)


def level_of(number, ceiling):
    depth_now = 1
    while number % 2 == 0 and depth_now <= ceiling:
        number = number // 2
        depth_now = depth_now + 1
    return depth_now


def space_table(levels):
    period = 2**levels
    band_table = np.zeros((period * period, 3 * levels + 1), np.float32)
    for row_pos in range(period):
        for col_pos in range(period):
            row_level = level_of(row_pos, levels)
            col_level = level_of(col_pos, levels)
            finest = min(row_level, col_level)
            if finest > levels:
                column = 3 * levels
            elif row_level == col_level:
                column = 3 * (finest - 1) + 2
            elif row_level == finest:
                column = 3 * (finest - 1)
            else:
                column = 3 * (finest - 1) + 1
            band_table[row_pos * period + col_pos, column] = 1.0
    return band_table


def time_table(levels):
    period = 2**levels
    band_table = np.zeros((period, levels + 1), np.float32)
    for number in range(period):
        band_table[number, level_of(number, levels) - 1] = 1.0
    return band_table


def band_sums(coeffs, first_frame, levels_s, levels_t):
    period = 2**levels_s
    frame_count, row_count, col_count = coeffs.shape
    square = coeffs * coeffs
    row_folded = square.reshape(frame_count, row_count // period, period, col_count).sum(axis=1)
    column_phase = np.arange(col_count) % period
    selector = jnp.asarray((column_phase[:, None] == np.arange(period)[None, :]).astype(np.float32))
    pattern = jnp.dot(row_folded, selector, precision=lax.Precision.HIGHEST)
    pattern = pattern.reshape(frame_count, period * period)
    per_frame = jnp.dot(
        pattern, jnp.asarray(space_table(levels_s), jnp.float32), precision=lax.Precision.HIGHEST
    )
    time_period = 2**levels_t
    position = (first_frame + jnp.arange(frame_count, dtype=jnp.int32)) % time_period
    onehot = (position[:, None] == jnp.arange(time_period, dtype=jnp.int32)[None, :]).astype(
        jnp.float32
    )
    frame_band = jnp.dot(
        onehot, jnp.asarray(time_table(levels_t), jnp.float32), precision=lax.Precision.HIGHEST
    )
    return jnp.dot(frame_band.T, per_frame, precision=lax.Precision.HIGHEST)


def band_means(totals, frames_all, rows_all, cols_all, levels_s, levels_t):
    space_share = space_table(levels_s).sum(0) / float((2**levels_s) ** 2)
    time_share = time_table(levels_t).sum(0) / float(2**levels_t)
    counts = (
        float(frames_all) * float(rows_all) * float(cols_all) * np.outer(time_share, space_share)
    )
    return totals / jnp.asarray(counts, jnp.float32)


def shards(footage):
    frames_dev = footage.shape[0]
    planes = spatial_inplace(footage, SLEVELS)
    temporal_out = temporal(
        lax.all_to_all(planes, "frame", split_axis=1, concat_axis=0, tiled=True), TLEVELS
    )
    coeffs = lax.all_to_all(temporal_out, "frame", split_axis=0, concat_axis=1, tiled=True)
    totals = band_sums(coeffs, lax.axis_index("frame") * frames_dev, SLEVELS, TLEVELS)
    totals = lax.psum(totals, ("frame", "row"))
    means = band_means(
        totals,
        frames_dev * lax.axis_size("frame"),
        coeffs.shape[1] * lax.axis_size("row"),
        coeffs.shape[2],
        SLEVELS,
        TLEVELS,
    )
    return (coeffs, means)


def solution(mesh):
    return jax.shard_map(
        shards,
        mesh=mesh,
        in_specs=(P("frame", "row", None),),
        out_specs=(P("frame", "row", None), P()),
        check_vma=False,
    )
```

profile of v0, /device:TPU:14, one launch (start us, length us, event | category | flops | bytes accessed | tf_op | source)
XLA Modules:
  0.0 669.8 jit_solution(6688530232217569210)
XLA Ops:
  0.6 31.4 %convolution_bitcast_fusion = f32[4,512,1024]{2,1,0:T(8,128)} fusion(f32[1024,1024,1]{1,0,2:T(8,128)} %constant.85, f32[4,512,1024]{2,1,0:T(8,128)} %param.8), kind=kOutput, calls=%fused_computation.26 | convolution fusion | flops 25769803776 | bytes 20971520 | tf_op jit(solution)/shard_map/dot_general | solution.py:81
  32.0 10.6 %reshape.40 = f32[4,256,2,1024]{3,2,1,0:T(2,128)} reshape(f32[4,512,1024]{2,1,0:T(8,128)} %convolution_bitcast_fusion) | data formatting | bytes 16777216 | tf_op jit(solution)/shard_map/reshape | solution.py:82
  42.6 10.7 %fusion.50 = (f32[4,256,1,1024]{3,2,1,0:T(1,128)}, f32[4,256,1,1024]{3,2,1,0:T(1,128)S(1)}) fusion(f32[4,256,2,1024]{3,2,1,0:T(2,128)} %reshape.40), kind=kLoop, calls=%fused_computation.109 | loop fusion | bytes 16777216 | tf_op jit(solution)/shard_map/slice | solution.py:83
  57.4 2.5 slice.290
  60.8 7.3 %fusion.1 = f32[4,256,1024]{2,1,0:T(8,128)S(1)} fusion(f32[4,1,1024]{2,1,0:T(1,128)S(1)} %broadcast_select_fusion.1, f32[4,255,1024]{2,1,0:T(8,128)} %slice.290, f32[4,256,1,1024]{3,2,1,0:T(1,128)} %get-tuple-element.8, f32[4,256,1,1024]{3,2,1,0:T(1,128)} %copy-done.2), kind=kLoop, calls=%fused_computation.4 | loop fusion | flops 4194304 | bytes 16777216 | tf_op jit(solution)/shard_map/add | solution.py:52
  70.2 2.7 collective-permute-start.1
  74.3 6.8 %fusion.3 = f32[4,256,1024]{2,1,0:T(8,128)S(1)} fusion(f32[4,256,1024]{2,1,0:T(8,128)} %copy-done, f32[4,255,1024]{2,1,0:T(8,128)} %bitcast.99, f32[4,1,1024]{2,1,0:T(1,128)S(1)} %broadcast_select_fusion.3, f32[4,256,1,1024]{3,2,1,0:T(1,128)} %copy-done.2), kind=kLoop, calls=%fused_computation.7 | loop fusion | flops 4194304 | bytes 16777216 | tf_op jit(solution)/shard_map/add | solution.py:53
  82.7 2.5 slice.296
  85.2 5.8 broadcast_multiply_fusion
  91.0 3.0 collective-permute-start.3
  98.5 4.8 fusion.13
  103.4 2.5 reshape.41
  115.9 2.5 pad_maximum_fusion.3
  118.4 5.4 copy.49
  124.4 3.3 collective-permute-start.7
  138.1 2.9 collective-permute-start.9
  156.8 2.4 copy.47
  159.2 3.9 stack_reshape.35
  163.1 4.2 pad_maximum_fusion.2
  167.3 5.5 copy.48
  172.9 8.8 %pad_maximum_fusion = f32[4,256,2,1024]{1,0,3,2:T(4,128)} fusion(f32[4,256,1,1024]{1,0,3,2:T(4,128)} %bitcast.112, f32[4,256,1,1024]{1,0,3,2:T(4,128)} %bitcast.113), kind=kLoop, calls=%fused_computation | loop fusion | flops 2097152 | bytes 16777216 | tf_op jit(solution)/shard_map/stack | solution.py:90
  181.7 11.4 %copy.50 = f32[4,256,2,1024]{3,0,2,1:T(4,128)} copy(f32[4,256,2,1024]{1,0,3,2:T(4,128)} %pad_maximum_fusion) | data formatting | bytes 16777216 | tf_op jit(solution)/shard_map/stack | solution.py:90
  193.1 189.2 %all_to_all.36 = f32[4,512,1024]{2,0,1:T(4,128)S(1)} all-to-all(f32[4,512,1024]{2,0,1:T(4,128)} %bitcast.104), channel_id=1, replica_groups=mesh['frame'=16,'row'=2] {'frame'}, dimensions={1} | all-to-all | bytes 16777216 | tf_op jit(solution)/shard_map/all_to_all | solution.py:187
  382.3 4.9 copy.51
  401.4 4.2 copy.55
  405.7 6.7 all-to-all-start.1
  412.6 184.9 %all-to-all-done.1 = f32[64,32,1024]{2,1,0:T(8,128)} async-done(((f32[64,32,1024]{2,1,0:T(8,128)}), f32[64,32,1024]{2,1,0:T(8,128)}, u32[]{:S(2)}, u32[]{:S(2)}) %all-to-all-start.1) | async-done | bytes 8388640 | tf_op jit(solution)/shard_map/all_to_all | solution.py:189
  597.5 12.0 %mul.203 = f32[4,16,32,1024]{3,2,0,1:T(8,128)} multiply(f32[4,16,32,1024]{3,2,0,1:T(8,128)} %bitcast.39, f32[4,16,32,1024]{3,2,0,1:T(8,128)} %bitcast.39) | non-fusion elementwise | flops 2097152 | bytes 25165824 | tf_op jit(solution)/shard_map/mul | solution.py:154
  609.5 8.6 %copy.56 = f32[4,16,32,1024]{3,2,1,0:T(8,128)} copy(f32[4,16,32,1024]{3,2,0,1:T(8,128)} %bitcast.39) | data formatting | bytes 16777216 | tf_op jit(solution)/shard_map/all_to_all | solution.py:189
  618.1 4.1 copy.57
  622.2 3.9 reduce_sum.9
  626.8 41.9 %psum.7 = f32[4,10]{1,0:T(4,128)S(1)} all-reduce(f32[4,10]{1,0:T(4,128)S(1)} %fusion.56), channel_id=1, replica_groups=mesh['frame'=16,'row'=2] {'frame','row'}, use_global_device_ids=true, to_apply=%region_1.2 | all-reduce | flops 40 | bytes 320 | tf_op jit(solution)/shard_map/psum | solution.py:191
  (154 shorter events, 66.4 us)
Async XLA Ops:
  53.3 2.0 copy-start.2
  55.4 2.0 copy-start.4
  55.4 4.5 collective-permute-start
  68.2 2.0 copy-start
  70.2 3.2 collective-permute-start.1
  81.1 4.1 copy-start.1
  81.1 4.1 collective-permute-start.2
  91.0 3.9 collective-permute-start.3
  94.9 3.6 copy-start.14
  96.5 2.0 copy-start.5
  107.5 5.9 copy-start.7
  107.6 3.3 collective-permute-start.4
  111.3 2.9 collective-permute-start.5
  114.6 9.3 %collective-permute-start.6 = (f32[4,1,512]{2,1,0:T(1,128)S(1)}, f32[4,1,512]{2,1,0:T(1,128)S(1)}, u32[]{:S(2)}, u32[]{:S(2)}) collective-permute-start(f32[4,1,512]{2,1,0:T(1,128)S(1)} %slice.313), channel_id=1, source_target_pairs={{1,0},{3,2},{5,4},{7,6},{9,8},{11,10},{13,12},{15,14},{17,16},{19,... | collective-permute-start | bytes 24584 | tf_op jit(solution)/shard_map/ppermute | solution.py:19
  123.8 3.9 copy-start.6
  124.4 5.3 copy-start.15
  124.4 4.8 collective-permute-start.7
  129.7 7.2 %copy-start.9 = (f32[4,128,512]{2,1,0:T(8,128)}, f32[4,128,512]{2,1,0:T(8,128)S(1)}, u32[]{:S(2)}) copy-start(f32[4,128,512]{2,1,0:T(8,128)S(1)} %fusion.27) | copy-start | bytes 3145732
  132.8 3.8 collective-permute-start.8
  135.7 5.3 copy-start.12
  135.7 5.3 copy-start.13
  138.1 4.0 collective-permute-start.9
  142.3 4.1 collective-permute-start.10
  147.0 3.6 collective-permute-start.11
  150.9 2.1 copy-start.11
  159.2 3.9 copy-start.8
  405.7 6.7 copy-start.19
  405.7 191.8 %all-to-all-start.1 = ((f32[64,32,1024]{2,1,0:T(8,128)}), f32[64,32,1024]{2,1,0:T(8,128)}, u32[]{:S(2)}, u32[]{:S(2)}) async-start(f32[64,32,1024]{2,1,0:T(8,128)} %bitcast.102), calls=%async_computation.1 | async-start | bytes 16777216 | tf_op jit(solution)/shard_map/all_to_all | solution.py:189
  609.5 8.6 %copy-start.3 = (f32[4,16,32,1024]{3,2,0,1:T(8,128)S(1)}, f32[4,16,32,1024]{3,2,0,1:T(8,128)}, u32[]{:S(2)}) copy-start(f32[4,16,32,1024]{3,2,0,1:T(8,128)} %mul.203) | copy-start | bytes 25165828
  622.2 3.9 copy-start.17
  622.2 4.3 copy-start.16
  622.2 46.5 %copy-start.18 = (f32[4,10]{1,0:T(4,128)S(1)}, f32[4,10]{1,0:T(4,128)}, u32[]{:S(2)}) copy-start(f32[4,10]{1,0:T(4,128)} %constant.84) | copy-start | bytes 484
  (1 other events, 2.0 us)
where the time goes:
time: 680 us; the launch traced here: 670 us
  blocking collectives  231 us (34%)
  waiting for transfers between devices  192 us (28%)
  local copies, waits for them, and re-layouts  105 us (15%)
  other arithmetic  70.7 us (10%)
  matrix products  37.5 us (6%)
  starting transfers between devices  31 us (5%)
    all_to_all x1, blocking collectives, shards(): lax.all_to_all(planes, 'frame', split_axis=1, concat_axis=0, tiled=True)  189 us
    all_to_all x1, waiting for transfers between devices, shards(): lax.all_to_all(temporal_out, 'frame', split_axis=0, concat_axis=1, tiled=...  185 us
    psum x1, blocking collectives, shards(): totals = lax.psum(totals, ('frame', 'row'))  41.9 us
    dot_general x3, matrix products, spatial_inplace(): jnp.dot(block, column_matrix(width), precision=lax.Precision.HIGHEST)  36.7 us
    another operation x15, local copies, waits for them, and re-layouts, weave_axis(): stacked = jnp.stack([even_part, odd_part], axis=along + 1)  27.3 us
    ppermute x12, starting transfers between devices, shifted(): return lax.ppermute(block, axis, route)  24.3 us
    another operation x3, local copies, waits for them, and re-layouts, spatial_inplace(): jnp.stack([upper_rows, bottom], axis=2)  14.1 us
  transfers between devices with their start and end apart: 13, of which 9 were waited for; matrix products, arithmetic and copies ran while one was open for 3% of the time, Pallas kernels for 0%

commit v1 on v0

--- a/solution.py
+++ b/solution.py
@@ -186,7 +186,12 @@
     temporal_out = temporal(
         lax.all_to_all(planes, "frame", split_axis=1, concat_axis=0, tiled=True), TLEVELS
     )
-    coeffs = lax.all_to_all(temporal_out, "frame", split_axis=0, concat_axis=1, tiled=True)
+    coeffs = jnp.concatenate(
+        lax.all_to_all(
+            jnp.stack(jnp.split(temporal_out, lax.axis_size("frame"), axis=0)), "frame", 0, 0
+        ),
+        axis=1,
+    )
     totals = band_sums(coeffs, lax.axis_index("frame") * frames_dev, SLEVELS, TLEVELS)
     totals = lax.psum(totals, ("frame", "row"))
     means = band_means(

time: 680 us -> 681 us (level)
  local copies, waits for them, and re-layouts: 105 us -> 115 us
  other arithmetic: 70.7 us -> 62.2 us
    unnamed x44 -> x57, local copies, waits for them, and re-layouts: 8.26 us -> 20.8 us
    all_to_all x1 -> x0, local copies, waits for them, and re-layouts: 8.59 us -> none  [shards(): lax.all_to_all(temporal_out, 'frame', split_axis=0, concat_axis=1, tiled=...]
    reshape x0 -> x1, local copies, waits for them, and re-layouts: none -> 8.45 us  [shards(): jnp.concatenate(lax.all_to_all(jnp.stack(jnp.split(temporal_out, lax.axis...]
    mul x1, other arithmetic: 12 us -> 4.35 us  [band_sums(): square = coeffs * coeffs]
    another operation x15 -> x14, local copies, waits for them, and re-layouts: 27.3 us -> 23.1 us  [weave_axis(): stacked = jnp.stack([even_part, odd_part], axis=along + 1)]
where the time goes in v1:
time: 681 us; the launch traced here: 671 us
  blocking collectives  231 us (34%)
  waiting for transfers between devices  192 us (28%)
  local copies, waits for them, and re-layouts  115 us (17%)
  other arithmetic  62.2 us (9%)
  matrix products  37.5 us (6%)
  starting transfers between devices  31 us (5%)
    all_to_all x1, blocking collectives, shards(): lax.all_to_all(planes, 'frame', split_axis=1, concat_axis=0, tiled=True)  189 us
    all_to_all x1, waiting for transfers between devices, shards(): lax.all_to_all(jnp.stack(jnp.split(temporal_out, lax.axis_size('frame'),...  185 us
    psum x1, blocking collectives, shards(): totals = lax.psum(totals, ('frame', 'row'))  41.9 us
    dot_general x3, matrix products, spatial_inplace(): jnp.dot(block, column_matrix(width), precision=lax.Precision.HIGHEST)  36.7 us
    ppermute x12, starting transfers between devices, shifted(): return lax.ppermute(block, axis, route)  24.3 us
    another operation x14, local copies, waits for them, and re-layouts, weave_axis(): stacked = jnp.stack([even_part, odd_part], axis=along + 1)  23.1 us
    unnamed x57, local copies, waits for them, and re-layouts  20.8 us
    another operation x3, local copies, waits for them, and re-layouts, spatial_inplace(): jnp.stack([upper_rows, bottom], axis=2)  14.1 us
  transfers between devices with their start and end apart: 13, of which 9 were waited for; matrix products, arithmetic and copies ran while one was open for 3% of the time, Pallas kernels for 0%

profile of v1, /device:TPU:14, one launch (start us, length us, event | category | flops | bytes accessed | tf_op | source)
XLA Modules:
  0.0 671.3 jit_solution(5780232659680300098)
XLA Ops:
  0.6 31.4 %convolution_bitcast_fusion = f32[4,512,1024]{2,1,0:T(8,128)} fusion(f32[1024,1024,1]{1,0,2:T(8,128)} %constant.85, f32[4,512,1024]{2,1,0:T(8,128)} %param.8), kind=kOutput, calls=%fused_computation.55 | convolution fusion | flops 25769803776 | bytes 20971520 | tf_op jit(solution)/shard_map/dot_general | solution.py:81
  32.0 10.7 %reshape.76 = f32[4,256,2,1024]{3,2,1,0:T(2,128)} reshape(f32[4,512,1024]{2,1,0:T(8,128)} %convolution_bitcast_fusion) | data formatting | bytes 16777216 | tf_op jit(solution)/shard_map/reshape | solution.py:82
  42.6 10.7 %fusion.65 = (f32[4,256,1,1024]{3,2,1,0:T(1,128)}, f32[4,256,1,1024]{3,2,1,0:T(1,128)S(1)}) fusion(f32[4,256,2,1024]{3,2,1,0:T(2,128)} %reshape.76), kind=kLoop, calls=%fused_computation.171 | loop fusion | bytes 16777216 | tf_op jit(solution)/shard_map/slice | solution.py:83
  57.4 2.5 slice.306
  60.9 7.3 %fusion.1 = f32[4,256,1024]{2,1,0:T(8,128)S(1)} fusion(f32[4,1,1024]{2,1,0:T(1,128)S(1)} %broadcast_select_fusion.1, f32[4,255,1024]{2,1,0:T(8,128)} %slice.306, f32[4,256,1,1024]{3,2,1,0:T(1,128)} %get-tuple-element.24, f32[4,256,1,1024]{3,2,1,0:T(1,128)} %copy-done.2), kind=kLoop, calls=%fused_computation.33 | loop fusion | flops 4194304 | bytes 16777216 | tf_op jit(solution)/shard_map/add | solution.py:52
  70.2 2.7 collective-permute-start.1
  74.3 6.8 %fusion.3 = f32[4,256,1024]{2,1,0:T(8,128)S(1)} fusion(f32[4,256,1024]{2,1,0:T(8,128)} %copy-done, f32[4,255,1024]{2,1,0:T(8,128)} %bitcast.147, f32[4,1,1024]{2,1,0:T(1,128)S(1)} %broadcast_select_fusion.3, f32[4,256,1,1024]{3,2,1,0:T(1,128)} %copy-done.2), kind=kLoop, calls=%fused_computation.36 | loop fusion | flops 4194304 | bytes 16777216 | tf_op jit(solution)/shard_map/add | solution.py:53
  82.8 2.5 slice.312
  85.3 5.8 broadcast_multiply_fusion
  91.1 3.0 collective-permute-start.3
  98.6 4.8 fusion.13
  103.4 2.5 reshape.77
  116.0 2.5 pad_maximum_fusion.2
  118.5 5.5 copy.82
  124.5 3.3 collective-permute-start.7
  138.2 2.9 collective-permute-start.9
  147.1 2.1 collective-permute-start.11
  156.9 2.4 copy.80
  159.3 3.9 stack_reshape.35
  163.2 4.2 pad_maximum_fusion.1
  167.5 5.5 copy.81
  173.0 8.8 %pad_maximum_fusion = f32[4,256,2,1024]{1,0,3,2:T(4,128)} fusion(f32[4,256,1,1024]{1,0,3,2:T(4,128)} %bitcast.160, f32[4,256,1,1024]{1,0,3,2:T(4,128)} %bitcast.161), kind=kLoop, calls=%fused_computation.30 | loop fusion | flops 2097152 | bytes 16777216 | tf_op jit(solution)/shard_map/stack | solution.py:90
  181.8 11.4 %copy.83 = f32[4,256,2,1024]{3,0,2,1:T(4,128)} copy(f32[4,256,2,1024]{1,0,3,2:T(4,128)} %pad_maximum_fusion) | data formatting | bytes 16777216 | tf_op jit(solution)/shard_map/stack | solution.py:90
  193.2 189.2 %all_to_all.23 = f32[4,512,1024]{2,0,1:T(4,128)S(1)} all-to-all(f32[4,512,1024]{2,0,1:T(4,128)} %bitcast.152), channel_id=1, replica_groups=mesh['frame'=16,'row'=2] {'frame'}, dimensions={1} | all-to-all | bytes 16777216 | tf_op jit(solution)/shard_map/all_to_all | solution.py:187
  382.4 4.9 copy.84
  414.9 6.7 all-to-all-start.1
  421.7 185.0 %all-to-all-done.1 = f32[16,4,32,1024]{3,2,1,0:T(8,128)} async-done(((f32[16,4,32,1024]{3,2,1,0:T(8,128)}), f32[16,4,32,1024]{3,2,1,0:T(8,128)}, u32[]{:S(2)}, u32[]{:S(2)}) %all-to-all-start.1) | async-done | bytes 8388640 | tf_op jit(solution)/shard_map/all_to_all | solution.py:190
  606.7 4.4 bitcast_multiply_fusion
  611.1 4.2 copy.105
  615.3 3.9 reduce_sum.9
  619.9 41.9 %psum.7 = f32[4,10]{1,0:T(4,128)S(1)} all-reduce(f32[4,10]{1,0:T(4,128)S(1)} %fusion.71), channel_id=1, replica_groups=mesh['frame'=16,'row'=2] {'frame','row'}, use_global_device_ids=true, to_apply=%region_1.2 | all-reduce | flops 40 | bytes 320 | tf_op jit(solution)/shard_map/psum | solution.py:196
  661.8 8.5 %copy.104 = f32[4,16,32,1024]{3,2,1,0:T(8,128)} copy(f32[4,16,32,1024]{3,2,0,1:T(8,128)} %bitcast.53) | data formatting | bytes 16777216 | tf_op jit(solution)/shard_map/reshape | solution.py:189
  (184 shorter events, 77.5 us)
Async XLA Ops:
  53.3 2.1 copy-start.2
  55.4 2.0 copy-start.3
  55.4 4.5 collective-permute-start
  68.2 2.0 copy-start
  70.2 3.2 collective-permute-start.1
  81.2 4.1 copy-start.1
  81.2 4.1 collective-permute-start.2
  91.1 3.9 collective-permute-start.3
  95.0 3.6 copy-start.13
  96.6 2.0 copy-start.4
  107.5 5.9 copy-start.6
  107.7 3.3 collective-permute-start.4
  111.4 2.9 collective-permute-start.5
  114.7 9.3 %collective-permute-start.6 = (f32[4,1,512]{2,1,0:T(1,128)S(1)}, f32[4,1,512]{2,1,0:T(1,128)S(1)}, u32[]{:S(2)}, u32[]{:S(2)}) collective-permute-start(f32[4,1,512]{2,1,0:T(1,128)S(1)} %slice.329), channel_id=1, source_target_pairs={{1,0},{3,2},{5,4},{7,6},{9,8},{11,10},{13,12},{15,14},{17,16},{19,... | collective-permute-start | bytes 24584 | tf_op jit(solution)/shard_map/ppermute | solution.py:19
  123.9 3.9 copy-start.5
  124.5 5.3 copy-start.14
  124.5 4.8 collective-permute-start.7
  129.8 7.2 %copy-start.8 = (f32[4,128,512]{2,1,0:T(8,128)}, f32[4,128,512]{2,1,0:T(8,128)S(1)}, u32[]{:S(2)}) copy-start(f32[4,128,512]{2,1,0:T(8,128)S(1)} %fusion.27) | copy-start | bytes 3145732
  132.9 3.8 collective-permute-start.8
  135.7 5.3 copy-start.11
  135.8 5.3 copy-start.12
  138.2 4.0 collective-permute-start.9
  141.7 2.0 copy-start.9
  142.4 4.1 collective-permute-start.10
  147.1 3.6 collective-permute-start.11
  151.0 2.1 copy-start.10
  159.3 3.9 copy-start.7
  414.9 6.7 copy-start.18
  414.9 191.8 %all-to-all-start.1 = ((f32[16,4,32,1024]{3,2,1,0:T(8,128)}), f32[16,4,32,1024]{3,2,1,0:T(8,128)}, u32[]{:S(2)}, u32[]{:S(2)}) async-start(f32[16,4,32,1024]{3,2,1,0:T(8,128)} %bitcast_dynamic-update-slice_fusion), calls=%async_computation.1 | async-start | bytes 16777216 | tf_op jit(solution)/shard_map/all_to_all | solution.py:190
  615.3 3.9 copy-start.16
  615.3 4.2 copy-start.15
  661.8 8.5 %copy-start.17 = (f32[4,10]{1,0:T(4,128)S(1)}, f32[4,10]{1,0:T(4,128)}, u32[]{:S(2)}) copy-start(f32[4,10]{1,0:T(4,128)} %constant.84) | copy-start | bytes 484
